TPU v7x, 256 devices: a whole 4x4x8 slice. The times are simulated.
256 devices in a mesh: rows: 64 (over z, y, core), panel: 4 (over x).
Axes of the slice: x: 4, y: 4, z: 8, core: 2. Of those that a mesh axis runs over, the one named last changes fastest.
Arguments:
- pair_block: bfloat16 [2048, 16384], P('rows', 'panel'), may hold values from -6 to 6
- resolvent: float32 [16384, 16384], P('panel', 'rows'), may hold values from -0.046875 to 0.046875
- virt_coef: bfloat16 [1024, 11200], P('rows', 'panel'), may hold values from -0.1875 to 0.1875
- slot_row: int32 [2048], replicated, may hold values from 0 to 2047, each once
Outputs:
- backward: float32 [2, 11200, 16384], P(None, 'panel', 'rows')
Inputs may be any that keep to these rules, and one draw needn't show every extreme that they name: `slot_row`: every pair row appears exactly once.
All inputs are finite; a program needn't handle non-finite values.
Results may differ from a plain program's by a relative error of at most 0.0041.
Values may be sent and summed in bfloat16 or wider, within the bound.
A program may use at most 128 MiB of HBM per device.

v0:
```python
import jax
import jax.numpy as jnp
from jax import lax
from jax.sharding import PartitionSpec as P

OCC_B = 2


def body(pair_block, resolvent, virt_coef, slot_row):
    resolvent_round = resolvent.astype(jnp.bfloat16)
    gathered = None
    partial_sum = jnp.dot(
        lax.all_gather(pair_block, "rows", axis=0, tiled=True),
        resolvent_round,
        preferred_element_type=jnp.float32,
    )
    gathered = lax.psum(partial_sum, "panel").astype(jnp.bfloat16)
    grouped = jnp.take(gathered, slot_row, axis=0)
    grouped = grouped.reshape(OCC_B, slot_row.shape[0] // OCC_B, gathered.shape[1])
    coef_all = lax.all_gather(virt_coef, "rows", axis=0, tiled=True)
    return jnp.einsum("am,oac->omc", coef_all, grouped, preferred_element_type=jnp.float32)


def solution(mesh):
    placed = (P("rows", "panel"), P("panel", "rows"), P("rows", "panel"), P())
    return jax.shard_map(
        body, mesh=mesh, in_specs=placed, out_specs=P(None, "panel", "rows"), check_vma=False
    )
```

profile of v0, /device:TPU:1, one launch (start us, length us, event | category | flops | bytes accessed | tf_op | source)
XLA Modules:
  0.0 209.5 jit_solution(6740521300446435897)
XLA Ops:
  6.5 0.0 all-gather.3.cloned.1.call-start
  6.5 0.7 all-gather.3.cloned.1.call-update
  7.3 0.0 all-gather.5.cloned.1.call-start
  7.3 0.7 all-gather.5.cloned.1.call-update
  8.0 0.7 compare_and_fusion
  8.7 0.7 fusion.10
  9.4 104.2 %all-gather.3.cloned.1.call-done = bf16[2048,4096]{1,0:T(8,128)(2,1)} async-done(((bf16[32,4096]{1,0:T(8,128)(2,1)}), bf16[2048,4096]{1,0:T(8,128)(2,1)}) %all-gather.3.cloned.1.call-update) | async-done | bytes 16777232 | tf_op jit(solution)/shard_map/all_gather | solution.py:13
  113.6 9.3 %fusion.5 = f32[2048,256]{1,0:T(8,128)S(1)} fusion(bf16[2048,4096]{1,0:T(8,128)(2,1)} %all-gather.3.cloned.1.call-done, f32[4096,256]{1,0:T(8,128)} %param.5), kind=kOutput, calls=%fused_computation.4 | convolution fusion | flops 4296015872 | bytes 23068672 | tf_op jit(solution)/shard_map/dot_general | solution.py:12
  122.9 42.3 %all-reduce.1 = bf16[2048,256]{1,0:T(8,128)(2,1)S(1)} all-reduce(f32[2048,256]{1,0:T(8,128)S(1)} %fusion.5), channel_id=1, replica_groups=mesh['rows'=64,'panel'=4] {'panel'}, use_global_device_ids=true, to_apply=%region_0.0 | all-reduce | flops 524288 | bytes 3145728 | tf_op jit(solution)/shard_map/psum | solution.py:17
  165.2 7.5 %gather_fusion = bf16[2048,256]{1,0:T(8,128)(2,1)S(1)} fusion(bf16[2048,256]{1,0:T(8,128)(2,1)S(1)} %all-reduce.1, s32[2048]{0:T(1024)S(1)} %fusion.10), kind=kCustom, calls=%fused_computation | custom fusion | bytes 2105344 | tf_op jit(solution)/shard_map/jit(_take)/gather | solution.py:18
  172.7 20.7 %all-gather.5.cloned.1.call-done = bf16[1024,2800]{1,0:T(8,128)(2,1)} async-done(((bf16[16,2800]{1,0:T(8,128)(2,1)}), bf16[1024,2800]{1,0:T(8,128)(2,1)}) %all-gather.5.cloned.1.call-update) | async-done | bytes 5734416 | tf_op jit(solution)/shard_map/all_gather | solution.py:20
  193.4 9.2 %fusion.2 = f32[2,2800,256]{2,1,0:T(8,128)} fusion(bf16[1024,2800]{1,0:T(8,128)(2,1)} %all-gather.5.cloned.1.call-done, bf16[2,1024,256]{2,1,0:T(8,128)(2,1)S(1)} %bitcast.9, pred[2,1024]{1,0:T(4,128)(4,1)S(1)} %broadcast_in_dim.14), kind=kOutput, calls=%fused_computation.3 | convolution fusion | flops 2936537088 | bytes 12519424 | tf_op jit(solution)/shard_map/am,oac->omc/dot_general | solution.py:21
  (1 shorter events, 0.0 us)
Async XLA Ops:
  6.5 107.1 %all-gather.3.cloned.1.call-start = ((), (), s32[]{:S(2)}) async-start(), calls=%async_computation | async-start | bytes 17039360 | tf_op jit(solution)/shard_map/all_gather | solution.py:13
  7.3 186.2 %all-gather.5.cloned.1.call-start = ((), (), s32[]{:S(2)}) async-start(), calls=%async_computation.1 | async-start | bytes 5857280 | tf_op jit(solution)/shard_map/all_gather | solution.py:20
Sparse Core Ops, SparseCore 0:
  10.1 103.4 all-gather.2
  116.3 77.0 all-gather.4
where the time goes:
time: 210 us; the launch traced here: 209 us
  waiting for transfers between devices  126 us (60%)
  blocking collectives  42.3 us (20%)
  matrix products  18.5 us (9%)
  between operations  13.4 us (6%)
  local copies, waits for them, and re-layouts  7.51 us (4%)
    all_gather x1, waiting for transfers between devices, body(): lax.all_gather(pair_block, 'rows', axis=0, tiled=True)  104 us
    psum x1, blocking collectives, body(): gathered = lax.psum(partial_sum, 'panel').astype(jnp.bfloat16)  42.3 us
    all_gather x1, waiting for transfers between devices, body(): coef_all = lax.all_gather(virt_coef, 'rows', axis=0, tiled=True)  20.7 us
    dot_general x1, matrix products, body(): jnp.dot(lax.all_gather(pair_block, 'rows', axis=0, tiled=True), resolvent...  9.32 us
    dot_general x1, matrix products, body(): jnp.einsum('am,oac->omc', coef_all, grouped, preferred_element_type=jnp.f...  9.22 us
    gather x1, local copies, waits for them, and re-layouts, body(): grouped = jnp.take(gathered, slot_row, axis=0)  7.5 us
  transfers between devices with their start and end apart: 2, of which 2 were waited for; matrix products, arithmetic and copies ran while one was open for 9% of the time, Pallas kernels for 0%

commit v1 on v0

--- a/solution.py
+++ b/solution.py
@@ -6,13 +6,16 @@
 OCC_B = 2
 
 
+def tiled_gather(x, axis, dim):
+    copies = jnp.concatenate([x] * lax.axis_size(axis), axis=dim)
+    return lax.all_to_all(copies, axis, dim, dim, tiled=True)
+
+
 def body(pair_block, resolvent, virt_coef, slot_row):
     resolvent_round = resolvent.astype(jnp.bfloat16)
     gathered = None
     partial_sum = jnp.dot(
-        lax.all_gather(pair_block, "rows", axis=0, tiled=True),
-        resolvent_round,
-        preferred_element_type=jnp.float32,
+        tiled_gather(pair_block, "rows", 0), resolvent_round, preferred_element_type=jnp.float32
     )
     gathered = lax.psum(partial_sum, "panel").astype(jnp.bfloat16)
     grouped = jnp.take(gathered, slot_row, axis=0)

time: 210 us -> 522 us (2.49)
  the two profiles are of different devices: /device:TPU:1 before, /device:TPU:48 now
where the time goes in v1:
time: 522 us; the launch traced here: 520 us
  waiting for transfers between devices  389 us (75%)
  local copies, waits for them, and re-layouts  45 us (9%)
  blocking collectives  42.5 us (8%)
  matrix products  18.6 us (4%)
  between operations  13.8 us (3%)
  starting transfers between devices  11.9 us (2%)
    all_to_all x1, waiting for transfers between devices, tiled_gather(): return lax.all_to_all(copies, axis, dim, dim, tiled=True)  388 us
    psum x1, blocking collectives, body(): gathered = lax.psum(partial_sum, 'panel').astype(jnp.bfloat16)  42.5 us
    unnamed x69, local copies, waits for them, and re-layouts  37.4 us
    all_to_all x1, starting transfers between devices, tiled_gather(): return lax.all_to_all(copies, axis, dim, dim, tiled=True)  11.9 us
  transfers between devices with their start and end apart: 2, of which 1 were waited for; matrix products, arithmetic and copies ran while one was open for 3% of the time, Pallas kernels for 0%

profile of v1, /device:TPU:48, one launch (start us, length us, event | category | flops | bytes accessed | tf_op | source)
XLA Modules:
  0.0 520.4 jit_solution(12080180762838295572)
XLA Ops:
  6.5 1.0 constant_dynamic-update-slice_fusion.63
  7.6 1.0 constant_dynamic-update-slice_fusion.62
  8.6 1.0 constant_dynamic-update-slice_fusion.61
  9.5 1.0 constant_dynamic-update-slice_fusion.60
  10.5 1.0 constant_dynamic-update-slice_fusion.59
  11.5 1.0 constant_dynamic-update-slice_fusion.58
  12.4 1.0 constant_dynamic-update-slice_fusion.57
  13.4 1.0 constant_dynamic-update-slice_fusion.56
  14.4 1.0 constant_dynamic-update-slice_fusion.55
  15.4 1.0 constant_dynamic-update-slice_fusion.54
  16.3 1.0 constant_dynamic-update-slice_fusion.53
  17.3 1.0 constant_dynamic-update-slice_fusion.52
  18.3 1.0 constant_dynamic-update-slice_fusion.51
  19.3 1.0 constant_dynamic-update-slice_fusion.50
  20.2 1.0 constant_dynamic-update-slice_fusion.49
  21.2 1.0 constant_dynamic-update-slice_fusion.48
  22.2 1.0 constant_dynamic-update-slice_fusion.47
  38.6 5.7 %copy-done.1 = bf16[2048,4096]{1,0:T(8,128)(2,1)} copy-done((bf16[2048,4096]{1,0:T(8,128)(2,1)}, bf16[2048,4096]{1,0:T(8,128)(2,1)S(1)}, u32[]{:S(2)}) %copy-start.1) | copy-done | bytes 16777240
  44.4 11.9 %all-to-all-start = ((bf16[64,32,4096]{2,1,0:T(8,128)(2,1)}), bf16[64,32,4096]{2,1,0:T(8,128)(2,1)}, u32[]{:S(2)}, u32[]{:S(2)}) async-start(bf16[64,32,4096]{2,1,0:T(8,128)(2,1)} %bitcast.11), calls=%async_computation | async-start | bytes 33554432 | tf_op jit(solution)/shard_map/all_to_all | solution.py:11
  57.0 387.9 %all-to-all-done = bf16[64,32,4096]{2,1,0:T(8,128)(2,1)} async-done(((bf16[64,32,4096]{2,1,0:T(8,128)(2,1)}), bf16[64,32,4096]{2,1,0:T(8,128)(2,1)}, u32[]{:S(2)}, u32[]{:S(2)}) %all-to-all-start) | async-done | bytes 16777248 | tf_op jit(solution)/shard_map/all_to_all | solution.py:11
  445.0 9.3 %fusion.5 = f32[2048,256]{1,0:T(8,128)S(1)} fusion(bf16[2048,4096]{1,0:T(8,128)(2,1)} %bitcast.1, f32[4096,256]{1,0:T(8,128)} %param.5), kind=kOutput, calls=%fused_computation.4 | convolution fusion | flops 4296015872 | bytes 23068672 | tf_op jit(solution)/shard_map/dot_general | solution.py:17
  454.3 42.5 %all-reduce.1 = bf16[2048,256]{1,0:T(8,128)(2,1)S(1)} all-reduce(f32[2048,256]{1,0:T(8,128)S(1)} %fusion.5), channel_id=1, replica_groups=mesh['rows'=64,'panel'=4] {'panel'}, use_global_device_ids=true, to_apply=%region_0.0 | all-reduce | flops 524288 | bytes 3145728 | tf_op jit(solution)/shard_map/psum | solution.py:20
  496.8 7.5 %gather_fusion = bf16[2048,256]{1,0:T(8,128)(2,1)S(1)} fusion(bf16[2048,256]{1,0:T(8,128)(2,1)S(1)} %all-reduce.1, s32[2048]{0:T(1024)S(1)} %fusion.10), kind=kCustom, calls=%fused_computation | custom fusion | bytes 2105344 | tf_op jit(solution)/shard_map/jit(_take)/gather | solution.py:21
  504.3 9.2 %fusion.2 = f32[2,2800,256]{2,1,0:T(8,128)} fusion(bf16[1024,2800]{1,0:T(8,128)(2,1)} %all-gather.2.cloned.1.call-done, bf16[2,1024,256]{2,1,0:T(8,128)(2,1)S(1)} %bitcast.12, pred[2,1024]{1,0:T(4,128)(4,1)S(1)} %broadcast_in_dim.14), kind=kOutput, calls=%fused_computation.3 | convolution fusion | flops 2936537088 | bytes 12519424 | tf_op jit(solution)/shard_map/am,oac->omc/dot_general | solution.py:24
  (58 shorter events, 16.0 us)
Async XLA Ops:
  6.5 31.2 %copy-start = (bf16[32,4096]{1,0:T(8,128)(2,1)S(1)}, bf16[32,4096]{1,0:T(8,128)(2,1)}, u32[]{:S(2)}) copy-start(bf16[32,4096]{1,0:T(8,128)(2,1)} %param.4) | copy-start | bytes 786436
  38.6 5.7 %copy-start.1 = (bf16[2048,4096]{1,0:T(8,128)(2,1)}, bf16[2048,4096]{1,0:T(8,128)(2,1)S(1)}, u32[]{:S(2)}) copy-start(bf16[2048,4096]{1,0:T(8,128)(2,1)S(1)} %constant_dynamic-update-slice_fusion) | copy-start | bytes 50331652
  44.4 12.6 %copy-start.2 = (s32[2048]{0:T(1024)S(1)}, s32[2048]{0:T(1024)}, u32[]{:S(2)}) copy-start(s32[2048]{0:T(1024)} %param.7) | copy-start | bytes 24580
  44.4 400.6 %all-to-all-start = ((bf16[64,32,4096]{2,1,0:T(8,128)(2,1)}), bf16[64,32,4096]{2,1,0:T(8,128)(2,1)}, u32[]{:S(2)}, u32[]{:S(2)}) async-start(bf16[64,32,4096]{2,1,0:T(8,128)(2,1)} %bitcast.11), calls=%async_computation | async-start | bytes 33554432 | tf_op jit(solution)/shard_map/all_to_all | solution.py:11
  56.2 448.1 %all-gather.2.cloned.1.call-start = ((), (), s32[]{:S(2)}) async-start(), calls=%async_computation.1 | async-start | bytes 5857280 | tf_op jit(solution)/shard_map/all_gather | solution.py:23
Sparse Core Ops, SparseCore 0:
  59.8 154.0 all-gather.1
